TPU v7x, 32 devices: a whole 2x2x4 slice. The times are simulated.
32 devices in a mesh: worker: 8 (over y, x, core), mp: 4 (over z).
Axes of the slice: x: 2, y: 2, z: 4, core: 2. Of those that a mesh axis runs over, the one named last changes fastest.
Arguments:
- gradients: float32 [8, 2097152], P('worker', 'mp'), may hold values from -100 to 100
- neighbours: int32 [8, 3], replicated, may hold values from 0 to 7, as said below
- winner: int32 [1], replicated, may hold values from 0 to 7
Outputs:
- scores: float32 [8], replicated
- aggregate: float32 [2097152], P(('mp', 'worker'))
Inputs may be any that keep to these rules, and one draw needn't show every extreme that they name: `neighbours`: row i lists 3 different workers, none of them equal to i.
All inputs are finite; a program needn't handle non-finite values.
Results may differ from a plain program's by a relative error of at most 0.0003.
Values may be sent and summed in bfloat16 or wider, within the bound.
A program may use at most 64 MiB of HBM per device.

v0:
```python
import functools

import jax
import jax.numpy as jnp
from jax import lax
from jax.experimental import pallas as pl
from jax.experimental.pallas import tpu as pltpu
from jax.sharding import PartitionSpec as P

MESH = pl.DeviceIdType.MESH
LANES = 128
CHUNKS = 4


def flip(index, offset, size):
    result, bit = 0, 1
    while bit < size:
        digit = (index // bit) % 2
        if (offset // bit) % 2:
            digit = 1 - digit
        result = result + digit * bit
        bit *= 2
    return result


def kernel(
    workers,
    planes,
    total_entries,
    nb_hbm,
    win_ref,
    g_ref,
    scores_ref,
    out_ref,
    nb_ref,
    stage,
    rounded,
    recv,
    rest,
    rest_in,
    rest_recv,
    relay,
    dist,
    part,
    zbuf,
    plane_part,
    pbuf,
    small_sem,
    load_sem,
    gsend,
    grecv,
    osend,
    orecv,
    ysend,
    yrecv,
    rsend,
    rrecv,
    zsend,
    zrecv,
    psend,
    precv,
):
    me = lax.axis_index("worker")
    plane = lax.axis_index("mp")
    core = me % 2
    chip = me // 2
    chips = workers // 2
    rows = stage.shape[1]
    span = rows // CHUNKS
    order = sorted(range(2, workers), key=lambda o: (bin(o // 2).count("1"), o % 2, o)) + [1, 0]
    near = [o for o in range(1, workers) if bin(o // 2).count("1") < 2]
    far = [o for o in order if bin(o // 2).count("1") >= 2]
    peer = [flip(me, o, workers) for o in range(workers)]

    barrier = pltpu.get_barrier_semaphore()
    for o in range(1, workers):
        pl.semaphore_signal(barrier, inc=1, device_id={"worker": peer[o]}, device_id_type=MESH)
    for z in range(1, planes):
        pl.semaphore_signal(
            barrier, inc=1, device_id={"mp": (plane + z) % planes}, device_id_type=MESH
        )

    def load(o):
        first = pl.multiple_of(peer[o] * rows, rows)
        return pltpu.make_async_copy(g_ref.at[pl.ds(first, rows), :], stage.at[o], load_sem.at[o])

    lists = pltpu.make_async_copy(nb_hbm, nb_ref, small_sem)
    load(order[0]).start()
    lists.start()
    for o in order[1:]:
        load(o).start()

    def gram_copy(o, c, slot):
        at = pl.ds(c * span, span)
        return pltpu.make_async_remote_copy(
            src_ref=rounded.at[o, at, :],
            dst_ref=recv.at[slot, at, :],
            send_sem=gsend.at[o, c],
            recv_sem=grecv.at[o, c],
            device_id={"worker": peer[o]},
            device_id_type=MESH,
        )

    def whole_copy(o, slot):
        return pltpu.make_async_remote_copy(
            src_ref=rounded.at[o],
            dst_ref=recv.at[slot],
            send_sem=gsend.at[o, 0],
            recv_sem=grecv.at[o, 0],
            device_id={"worker": peer[o]},
            device_id_type=MESH,
        )

    keep = jnp.where(win_ref[0] == me, 1.0, 0.0).astype(jnp.float32)
    block = 128

    def convert(o):
        parity = peer[o] % 2
        where = peer[o] // 2

        def one(step, carry):
            at = pl.ds(pl.multiple_of(step * block, block), block)
            x = stage[o, at, :]
            hi = x.astype(jnp.bfloat16)
            if o == 0:
                recv[me, at, :] = hi
            else:
                rounded[o, at, :] = hi
            rest[parity, where, at, :] = ((x - hi.astype(jnp.float32)) * keep).astype(jnp.bfloat16)
            return carry

        lax.fori_loop(0, rows // block, one, 0)

    def swap(ox):
        there = flip(chip, ox, chips)
        return pltpu.make_async_remote_copy(
            src_ref=rest.at[1 - core, there],
            dst_ref=rest_in.at[there],
            send_sem=osend.at[ox],
            recv_sem=orecv.at[ox],
            device_id={"worker": peer[1]},
            device_id_type=MESH,
        )

    def add_to_rest(there, first, count, other):
        def one(step, carry):
            at = pl.ds(pl.multiple_of(first + step * block, block), block)
            rest_in[there, at, :] = rest_in[there, at, :] + other(at)
            return carry

        lax.fori_loop(0, count // block, one, 0)

    def combine(ox):
        there = flip(chip, ox, chips)
        swap(ox).wait_recv()
        add_to_rest(there, 0, rows, lambda at: rest[core, there, at, :])

    split = chips == 4
    half = rows // 2

    def relay_copy(ox):
        return pltpu.make_async_remote_copy(
            src_ref=rest_in.at[flip(chip, 3, chips), pl.ds((ox - 1) * half, half), :],
            dst_ref=relay.at[ox - 1],
            send_sem=ysend.at[ox - 1],
            recv_sem=yrecv.at[ox - 1],
            device_id={"worker": peer[2 * ox]},
            device_id_type=MESH,
        )

    for n, o in enumerate(order):
        load(o).wait()
        convert(o)
        if n == 0:
            pl.semaphore_wait(barrier, workers - 1 + planes - 1)
        if o in near:
            whole_copy(o, me).start()
        if o % 2 == 1:
            swap(o // 2).start()

    for o in far[::2]:
        for c in range(CHUNKS):
            gram_copy(o, c, me).start()
            gram_copy(o + 1, c, me).start()
    if split:
        combine(3)
        relay_copy(1).start()
        relay_copy(2).start()
    for ox in range(chips):
        if not (split and ox == 3):
            combine(ox)

    def rest_copy(ox):
        return pltpu.make_async_remote_copy(
            src_ref=rest_in.at[flip(chip, ox, chips)],
            dst_ref=rest_recv.at[ox],
            send_sem=rsend.at[ox],
            recv_sem=rrecv.at[ox],
            device_id={"worker": peer[2 * ox]},
            device_id_type=MESH,
        )

    rest_order = sorted(range(1, chips), key=lambda ox: bin(ox).count("1"))
    if split:
        rest_order = [1, 2]

    pairs = [(i, k) for i in range(workers) for k in range(i, workers)]

    def gram(first, accs):
        def one(step, accs):
            at = pl.ds(pl.multiple_of(first + step * 16, 16), 16)
            xs = [recv[i, at, :].astype(jnp.float32) for i in range(workers)]
            lo = [x[:8] for x in xs]
            hi = [x[8:] for x in xs]
            return tuple(
                a + (lo[i] * lo[k] + hi[i] * hi[k]) for a, (i, k) in zip(accs, pairs)
            )

        return lax.fori_loop(0, span // 16, one, accs)

    accs = tuple(jnp.zeros((8, LANES), jnp.float32) for _ in pairs)
    for o in near:
        whole_copy(o, peer[o]).wait_recv()
    for c in range(CHUNKS):
        for o in far:
            gram_copy(o, c, peer[o]).wait_recv()
        accs = gram(c * span, accs)

    value = dict(zip(pairs, accs))
    for i, k in pairs:
        if i == k:
            dist[i * workers + i] = jnp.zeros((8, LANES), jnp.float32)
        else:
            d = value[i, i] + value[k, k] - 2.0 * value[i, k]
            dist[i * workers + k] = d
            dist[k * workers + i] = d
    lists.wait()
    for i in range(workers):
        s = dist[i * workers + nb_ref[0, i]]
        for j in range(1, nb_ref.shape[0]):
            s = s + dist[i * workers + nb_ref[j, i]]
        part[pl.ds(i, 1), :] = jnp.sum(s, axis=0, keepdims=True)

    def z_copy(z):
        return pltpu.make_async_remote_copy(
            src_ref=part,
            dst_ref=zbuf.at[z],
            send_sem=zsend.at[z],
            recv_sem=zrecv.at[z],
            device_id={"mp": (plane + z) % planes},
            device_id_type=MESH,
        )

    def p_copy(o):
        return pltpu.make_async_remote_copy(
            src_ref=plane_part,
            dst_ref=pbuf.at[o],
            send_sem=psend.at[o],
            recv_sem=precv.at[o],
            device_id={"worker": peer[o]},
            device_id_type=MESH,
        )

    for z in range(1, planes):
        z_copy(z).start()
    for ox in rest_order:
        if split:
            first = (ox - 1) * half
            relay_copy(ox).wait_recv()
            add_to_rest(
                flip(chip, 3 - ox, chips),
                first,
                half,
                lambda at, first=first, ox=ox: relay[
                    ox - 1, pl.ds(pl.multiple_of(at.start - first, block), block), :
                ],
            )
    for ox in rest_order:
        rest_copy(ox).start()
    total = part[...]
    for z in range(1, planes):
        z_copy(z).wait_recv()
        total = total + zbuf[z]
    plane_part[...] = total
    for o in range(1, workers):
        p_copy(o).start()

    for ox in rest_order:
        rest_copy(ox).wait_recv()

    def finish(step, carry):
        at = pl.ds(pl.multiple_of(step * block, block), block)
        low = rest_in[chip, at, :].astype(jnp.float32)
        for ox in rest_order:
            low = low + rest_recv[ox, at, :].astype(jnp.float32)
        out_ref[at, :] = recv[win_ref[0], at, :].astype(jnp.float32) + low
        return carry

    lax.fori_loop(0, rows // block, finish, 0)

    for o in range(1, workers):
        p_copy(o).wait_recv()
        total = total + pbuf[o]
    column = jnp.sum(total, axis=1, keepdims=True) / jnp.float32(total_entries)
    line = lax.broadcasted_iota(jnp.int32, (workers, LANES), 0)
    lane = lax.broadcasted_iota(jnp.int32, (workers, LANES), 1)
    scores_ref[...] = jnp.sum(
        jnp.where(line == lane, column, 0.0), axis=0, keepdims=True
    )[:, :workers]

    for ox in range(chips):
        swap(ox).wait_send()
    if split:
        relay_copy(1).wait_send()
        relay_copy(2).wait_send()
    for o in near:
        whole_copy(o, me).wait_send()
    for o in far:
        for c in range(CHUNKS):
            gram_copy(o, c, me).wait_send()
    for ox in rest_order:
        rest_copy(ox).wait_send()
    for z in range(1, planes):
        z_copy(z).wait_send()
    for o in range(1, workers):
        p_copy(o).wait_send()


def emit(scores_ref, block_ref, scores_out, block_out, sems):
    copies = [
        pltpu.make_async_copy(block_ref, block_out, sems.at[0]),
        pltpu.make_async_copy(scores_ref, scores_out, sems.at[1]),
    ]
    for copy in copies:
        copy.start()
    for copy in copies:
        copy.wait()


def solution(mesh):
    workers = mesh.shape["worker"]
    planes = mesh.shape["mp"]
    chips = workers // 2

    def body(gradients, neighbours, winner):
        length = gradients.shape[1]
        rows = length // (LANES * workers)
        entries = neighbours.shape[1] * length * planes
        bf16, f32 = jnp.bfloat16, jnp.float32
        dma = pltpu.SemaphoreType.DMA
        scores, aggregate = pl.pallas_call(
            functools.partial(kernel, workers, planes, entries),
            out_shape=(
                pltpu.VMEM((1, workers), f32),
                pltpu.VMEM((rows, LANES), f32),
            ),
            in_specs=[
                pl.BlockSpec(memory_space=pltpu.HBM),
                pl.BlockSpec(memory_space=pltpu.SMEM),
                pl.BlockSpec(memory_space=pltpu.HBM),
            ],
            out_specs=(
                pl.BlockSpec(memory_space=pltpu.VMEM),
                pl.BlockSpec(memory_space=pltpu.VMEM),
            ),
            scratch_shapes=[
                pltpu.SMEM(neighbours.shape[::-1], jnp.int32),
                pltpu.VMEM((workers, rows, LANES), f32),
                pltpu.VMEM((workers, rows, LANES), bf16),
                pltpu.VMEM((workers, rows, LANES), bf16),
                pltpu.VMEM((2, chips, rows, LANES), bf16),
                pltpu.VMEM((chips, rows, LANES), bf16),
                pltpu.VMEM((chips, rows, LANES), bf16),
                pltpu.VMEM((2, rows // 2, LANES), bf16),
                pltpu.VMEM((workers * workers, 8, LANES), f32),
                pltpu.VMEM((workers, LANES), f32),
                pltpu.VMEM((planes, workers, LANES), f32),
                pltpu.VMEM((workers, LANES), f32),
                pltpu.VMEM((workers, workers, LANES), f32),
                dma,
                dma((workers,)),
                dma((workers, CHUNKS)),
                dma((workers, CHUNKS)),
                dma((chips,)),
                dma((chips,)),
                dma((2,)),
                dma((2,)),
                dma((chips,)),
                dma((chips,)),
                dma((planes,)),
                dma((planes,)),
                dma((workers,)),
                dma((workers,)),
            ],
            compiler_params=pltpu.CompilerParams(
                collective_id=0, has_side_effects=True, vmem_limit_bytes=63_500_000
            ),
        )(neighbours.T, winner, gradients.reshape(length // LANES, LANES))
        scores, aggregate = pl.pallas_call(
            emit,
            out_shape=(
                jax.ShapeDtypeStruct(scores.shape, f32),
                jax.ShapeDtypeStruct(aggregate.shape, f32),
            ),
            in_specs=[pl.BlockSpec(memory_space=pltpu.VMEM)] * 2,
            out_specs=(pl.BlockSpec(memory_space=pl.ANY),) * 2,
            scratch_shapes=[dma((2,))],
            compiler_params=pltpu.CompilerParams(vmem_limit_bytes=8 * 1024 * 1024),
        )(scores, aggregate)
        return scores.reshape(workers), aggregate.reshape(rows * LANES)

    in_specs = (P("worker", "mp"), P(), P())
    out_specs = (P(), P(("mp", "worker")))
    return jax.shard_map(body, mesh=mesh, in_specs=in_specs, out_specs=out_specs, check_vma=False)
```

profile of v0, /device:TPU:0, one launch (start us, length us, event | category | flops | bytes accessed | tf_op | source)
XLA Modules:
  0.0 29.4 jit_solution(5601970575656383911)
XLA Ops:
  1.3 27.4 %shard_map.50 = (f32[1,8]{1,0:T(1,128)S(1)}, f32[512,128]{1,0:T(8,128)S(1)}) custom-call(s32[3,8]{1,0:T(4,128)} %bitcast.5, s32[1]{0:T(128)S(6)} %copy.5.win_ref, f32[4096,128]{1,0:T(8,128)} %bitcast.4), custom_call_target="tpu_custom_call" | custom-call | tf_op jit(solution)/shard_map/pallas_call | solution.py:351
  28.7 0.7 %shard_map.51 = (f32[1,8]{1,0:T(1,128)}, f32[512,128]{1,0:T(8,128)}) custom-call(f32[1,8]{1,0:T(1,128)S(1)} %get-tuple-element.6.scores_ref, f32[512,128]{1,0:T(8,128)S(1)} %get-tuple-element.7.block_ref), custom_call_target="tpu_custom_call" | custom-call | tf_op jit(solution)/shard_map/pallas_call | solution.py:399
where the time goes:
time: 29.6 us; the launch traced here: 29.4 us
  Pallas kernels  28.1 us (95%)
  between operations  1.28 us (4%)
    pallas_call x1, Pallas kernels, body(): pl.pallas_call(functools.partial(kernel, workers, planes, entries), out_s...  27.4 us
    pallas_call x1, Pallas kernels, body(): pl.pallas_call(emit, out_shape=(jax.ShapeDtypeStruct(scores.shape, f32),...  0.72 us

commit v1 on v0

v1 whole, which is shorter than its diff:
```python
import functools

import jax
import jax.numpy as jnp
from jax import lax
from jax.experimental import pallas as pl
from jax.experimental.pallas import tpu as pltpu
from jax.sharding import PartitionSpec as P

MESH = pl.DeviceIdType.MESH
LANES = 128
CHUNKS = 4


def flip(index, offset, size):
    result, bit = 0, 1
    while bit < size:
        digit = (index // bit) % 2
        if (offset // bit) % 2:
            digit = 1 - digit
        result = result + digit * bit
        bit *= 2
    return result


def kernel(
    workers,
    planes,
    total_entries,
    nb_hbm,
    win_ref,
    g_ref,
    scores_ref,
    out_ref,
    nb_ref,
    stage,
    rounded,
    recv,
    rest,
    rest_in,
    rest_recv,
    relay,
    dist,
    part,
    score_rows,
    small_sem,
    load_sem,
    gsend,
    grecv,
    osend,
    orecv,
    ysend,
    yrecv,
    rsend,
    rrecv,
    ssend,
    srecv,
):
    me = lax.axis_index("worker")
    plane = lax.axis_index("mp")
    core = me % 2
    chip = me // 2
    chips = workers // 2
    rows = stage.shape[1]
    span = rows // CHUNKS
    order = sorted(range(2, workers), key=lambda o: (-bin(o // 2).count("1"), o // 2, o % 2)) + [1, 0]
    peer = [flip(me, o, workers) for o in range(workers)]

    barrier = pltpu.get_barrier_semaphore()
    for o in range(1, workers):
        pl.semaphore_signal(barrier, inc=1, device_id={"worker": peer[o]}, device_id_type=MESH)
    for z in range(1, planes):
        pl.semaphore_signal(
            barrier, inc=1, device_id={"mp": (plane + z) % planes}, device_id_type=MESH
        )

    def load(o, c):
        first = pl.multiple_of(peer[o] * rows + c * span, span)
        return pltpu.make_async_copy(
            g_ref.at[pl.ds(first, span), :],
            stage.at[o, pl.ds(c * span, span), :],
            load_sem.at[o, c],
        )

    for c in range(CHUNKS):
        for o in order:
            load(o, c).start()
    lists = pltpu.make_async_copy(nb_hbm, nb_ref, small_sem)
    lists.start()

    def gram_copy(o, c, slot):
        at = pl.ds(c * span, span)
        return pltpu.make_async_remote_copy(
            src_ref=rounded.at[o, at, :],
            dst_ref=recv.at[slot, at, :],
            send_sem=gsend.at[o, c],
            recv_sem=grecv.at[o, c],
            device_id={"worker": peer[o]},
            device_id_type=MESH,
        )

    keep = jnp.where(win_ref[0] == me, 1.0, 0.0).astype(jnp.float32)

    def convert(o, c):
        at = pl.ds(c * span, span)
        x = stage[o, at, :]
        hi = x.astype(jnp.bfloat16)
        if o == 0:
            recv[me, at, :] = hi
        else:
            rounded[o, at, :] = hi
        low = ((x - hi.astype(jnp.float32)) * keep).astype(jnp.bfloat16)
        rest[peer[o] % 2, peer[o] // 2, at, :] = low

    def swap(ox):
        there = flip(chip, ox, chips)
        return pltpu.make_async_remote_copy(
            src_ref=rest.at[1 - core, there],
            dst_ref=rest_in.at[there],
            send_sem=osend.at[ox],
            recv_sem=orecv.at[ox],
            device_id={"worker": peer[1]},
            device_id_type=MESH,
        )

    def add_to_rest(there, at, other):
        rest_in[there, at, :] = rest_in[there, at, :] + other

    def combine(ox):
        there = flip(chip, ox, chips)
        swap(ox).wait_recv()
        for c in range(CHUNKS):
            at = pl.ds(c * span, span)
            add_to_rest(there, at, rest[core, there, at, :])

    split = chips == 4
    half = rows // 2

    def relay_copy(ox):
        return pltpu.make_async_remote_copy(
            src_ref=rest_in.at[flip(chip, 3, chips), pl.ds((ox - 1) * half, half), :],
            dst_ref=relay.at[ox - 1],
            send_sem=ysend.at[ox - 1],
            recv_sem=yrecv.at[ox - 1],
            device_id={"worker": peer[2 * ox]},
            device_id_type=MESH,
        )

    def rest_copy(ox, n):
        at = pl.ds(n * half, half)
        return pltpu.make_async_remote_copy(
            src_ref=rest_in.at[flip(chip, ox, chips), at, :],
            dst_ref=rest_recv.at[ox, at, :],
            send_sem=rsend.at[ox, n],
            recv_sem=rrecv.at[ox, n],
            device_id={"worker": peer[2 * ox]},
            device_id_type=MESH,
        )

    rest_order = sorted(range(1, chips), key=lambda ox: bin(ox).count("1"))
    if split:
        rest_order = [1, 2]

    first = True
    for c in range(CHUNKS):
        for o in order:
            load(o, c).wait()
            convert(o, c)
            if first:
                pl.semaphore_wait(barrier, workers - 1 + planes - 1)
                first = False
            if o:
                gram_copy(o, c, me).start()
    for ox in range(chips):
        swap(ox).start()

    pairs = [(i, k) for i in range(workers) for k in range(i, workers)]

    def gram(first, accs):
        def one(step, accs):
            at = pl.ds(pl.multiple_of(first + step * 16, 16), 16)
            xs = [recv[i, at, :].astype(jnp.float32) for i in range(workers)]
            lo = [x[:8] for x in xs]
            hi = [x[8:] for x in xs]
            return tuple(
                a + (lo[i] * lo[k] + hi[i] * hi[k]) for a, (i, k) in zip(accs, pairs)
            )

        return lax.fori_loop(0, span // 16, one, accs)

    accs = tuple(jnp.zeros((8, LANES), jnp.float32) for _ in pairs)
    for c in range(CHUNKS):
        if c == CHUNKS - 1:
            for ox in reversed(range(chips)):
                combine(ox)
            if split:
                relay_copy(1).start()
                relay_copy(2).start()
        for o in order[:-1]:
            gram_copy(o, c, peer[o]).wait_recv()
        accs = gram(c * span, accs)

    value = dict(zip(pairs, accs))
    for i, k in pairs:
        if i == k:
            dist[i * workers + i] = jnp.zeros((8, LANES), jnp.float32)
        else:
            d = value[i, i] + value[k, k] - 2.0 * value[i, k]
            dist[i * workers + k] = d
            dist[k * workers + i] = d
    lists.wait()
    for i in range(workers):
        s = dist[i * workers + nb_ref[0, i]]
        for j in range(1, nb_ref.shape[0]):
            s = s + dist[i * workers + nb_ref[j, i]]
        part[pl.ds(i, 1), :] = jnp.sum(s, axis=0, keepdims=True)
    column = jnp.sum(part[...], axis=1, keepdims=True)
    line = lax.broadcasted_iota(jnp.int32, (workers, LANES), 0)
    lane = lax.broadcasted_iota(jnp.int32, (workers, LANES), 1)
    mine = plane * workers + me
    score_rows[mine] = jnp.sum(jnp.where(line == lane, column, 0.0), axis=0, keepdims=True)

    def score_copy(o, z):
        return pltpu.make_async_remote_copy(
            src_ref=score_rows.at[mine],
            dst_ref=score_rows.at[mine],
            send_sem=ssend,
            recv_sem=srecv,
            device_id={"worker": peer[o], "mp": (plane + z) % planes},
            device_id_type=MESH,
        )

    def all_scores():
        others = score_rows.at[pl.ds(0, workers * planes - 1)]
        return pltpu.make_async_remote_copy(
            src_ref=others,
            dst_ref=others,
            send_sem=ssend,
            recv_sem=srecv,
            device_id={"worker": peer[1], "mp": plane},
            device_id_type=MESH,
        )

    for o in order:
        for z in range(planes):
            if o or z:
                score_copy(o, z).start()

    if split:
        for ox in rest_order:
            rest_copy(ox, ox - 1).start()
        for ox in rest_order:
            relay_copy(ox).wait_recv()
            add_to_rest(flip(chip, 3 - ox, chips), pl.ds((ox - 1) * half, half), relay[ox - 1])
            rest_copy(3 - ox, ox - 1).start()
    else:
        for ox in rest_order:
            for n in range(2):
                rest_copy(ox, n).start()

    for n in range(2):
        for ox in rest_order:
            rest_copy(ox, n).wait_recv()

    for c in range(CHUNKS):
        at = pl.ds(c * span, span)
        low = rest_in[chip, at, :].astype(jnp.float32)
        for ox in rest_order:
            low = low + rest_recv[ox, at, :].astype(jnp.float32)
        out_ref[at, :] = recv[win_ref[0], at, :].astype(jnp.float32) + low

    all_scores().wait_recv()
    total = jnp.sum(score_rows[...], axis=0) / jnp.float32(total_entries)
    scores_ref[...] = total[:, :workers]

    all_scores().wait_send()
    for ox in range(chips):
        swap(ox).wait_send()
    if split:
        relay_copy(1).wait_send()
        relay_copy(2).wait_send()
    for o in order[:-1]:
        for c in range(CHUNKS):
            gram_copy(o, c, me).wait_send()
    for ox in rest_order:
        for n in range(2):
            rest_copy(ox, n).wait_send()


def emit(scores_ref, block_ref, scores_out, block_out, sems):
    copies = [
        pltpu.make_async_copy(block_ref, block_out, sems.at[0]),
        pltpu.make_async_copy(scores_ref, scores_out, sems.at[1]),
    ]
    for copy in copies:
        copy.start()
    for copy in copies:
        copy.wait()


def solution(mesh):
    workers = mesh.shape["worker"]
    planes = mesh.shape["mp"]
    chips = workers // 2

    def body(gradients, neighbours, winner):
        length = gradients.shape[1]
        rows = length // (LANES * workers)
        entries = neighbours.shape[1] * length * planes
        bf16, f32 = jnp.bfloat16, jnp.float32
        dma = pltpu.SemaphoreType.DMA
        scores, aggregate = pl.pallas_call(
            functools.partial(kernel, workers, planes, entries),
            out_shape=(
                pltpu.VMEM((1, workers), f32),
                pltpu.VMEM((rows, LANES), f32),
            ),
            in_specs=[
                pl.BlockSpec(memory_space=pltpu.HBM),
                pl.BlockSpec(memory_space=pltpu.SMEM),
                pl.BlockSpec(memory_space=pltpu.HBM),
            ],
            out_specs=(
                pl.BlockSpec(memory_space=pltpu.VMEM),
                pl.BlockSpec(memory_space=pltpu.VMEM),
            ),
            scratch_shapes=[
                pltpu.SMEM(neighbours.shape[::-1], jnp.int32),
                pltpu.VMEM((workers, rows, LANES), f32),
                pltpu.VMEM((workers, rows, LANES), bf16),
                pltpu.VMEM((workers, rows, LANES), bf16),
                pltpu.VMEM((2, chips, rows, LANES), bf16),
                pltpu.VMEM((chips, rows, LANES), bf16),
                pltpu.VMEM((chips, rows, LANES), bf16),
                pltpu.VMEM((2, rows // 2, LANES), bf16),
                pltpu.VMEM((workers * workers, 8, LANES), f32),
                pltpu.VMEM((workers, LANES), f32),
                pltpu.VMEM((workers * planes, 1, LANES), f32),
                dma,
                dma((workers, CHUNKS)),
                dma((workers, CHUNKS)),
                dma((workers, CHUNKS)),
                dma((chips,)),
                dma((chips,)),
                dma((2,)),
                dma((2,)),
                dma((chips, 2)),
                dma((chips, 2)),
                dma,
                dma,
            ],
            compiler_params=pltpu.CompilerParams(
                collective_id=0, has_side_effects=True, vmem_limit_bytes=63_500_000
            ),
        )(neighbours.T, winner, gradients.reshape(length // LANES, LANES))
        scores, aggregate = pl.pallas_call(
            emit,
            out_shape=(
                jax.ShapeDtypeStruct(scores.shape, f32),
                jax.ShapeDtypeStruct(aggregate.shape, f32),
            ),
            in_specs=[pl.BlockSpec(memory_space=pltpu.VMEM)] * 2,
            out_specs=(pl.BlockSpec(memory_space=pl.ANY),) * 2,
            scratch_shapes=[dma((2,))],
            compiler_params=pltpu.CompilerParams(vmem_limit_bytes=8 * 1024 * 1024),
        )(scores, aggregate)
        return scores.reshape(workers), aggregate.reshape(rows * LANES)

    in_specs = (P("worker", "mp"), P(), P())
    out_specs = (P(), P(("mp", "worker")))
    return jax.shard_map(body, mesh=mesh, in_specs=in_specs, out_specs=out_specs, check_vma=False)
```

time: 29.6 us -> 27.5 us (0.929)
  Pallas kernels: 28.1 us -> 26 us
    pallas_call x1, Pallas kernels: 27.4 us -> 25.3 us  [body(): pl.pallas_call(functools.partial(kernel, workers, planes, entries), out_s...]
where the time goes in v1:
time: 27.5 us; the launch traced here: 27.3 us
  Pallas kernels  26 us (95%)
  between operations  1.28 us (5%)
    pallas_call x1, Pallas kernels, body(): pl.pallas_call(functools.partial(kernel, workers, planes, entries), out_s...  25.3 us
    pallas_call x1, Pallas kernels, body(): pl.pallas_call(emit, out_shape=(jax.ShapeDtypeStruct(scores.shape, f32),...  0.72 us

profile of v1, /device:TPU:0, one launch (start us, length us, event | category | flops | bytes accessed | tf_op | source)
XLA Modules:
  0.0 27.3 jit_solution(14412718599006699642)
XLA Ops:
  1.3 25.3 %shard_map.50 = (f32[1,8]{1,0:T(1,128)S(1)}, f32[512,128]{1,0:T(8,128)S(1)}) custom-call(s32[3,8]{1,0:T(4,128)} %bitcast.5, s32[1]{0:T(128)S(6)} %copy.5.win_ref, f32[4096,128]{1,0:T(8,128)} %bitcast.4), custom_call_target="tpu_custom_call" | custom-call | tf_op jit(solution)/shard_map/pallas_call | solution.py:312
  26.6 0.7 %shard_map.51 = (f32[1,8]{1,0:T(1,128)}, f32[512,128]{1,0:T(8,128)}) custom-call(f32[1,8]{1,0:T(1,128)S(1)} %get-tuple-element.6.scores_ref, f32[512,128]{1,0:T(8,128)S(1)} %get-tuple-element.7.block_ref), custom_call_target="tpu_custom_call" | custom-call | tf_op jit(solution)/shard_map/pallas_call | solution.py:356

commit v2 on v1

--- a/solution.py
+++ b/solution.py
@@ -9,7 +9,9 @@
 
 MESH = pl.DeviceIdType.MESH
 LANES = 128
-CHUNKS = 4
+CUTS = (0, 2, 4, 6, 8)
+PIECES = 2
+EARLY = ((), (1, 2), ())
 
 
 def flip(index, offset, size):
@@ -55,6 +57,9 @@
     rrecv,
     ssend,
     srecv,
+    hello,
+    chip_hello,
+    lines,
 ):
     me = lax.axis_index("worker")
     plane = lax.axis_index("mp")
@@ -62,47 +67,94 @@
     chip = me // 2
     chips = workers // 2
     rows = stage.shape[1]
-    span = rows // CHUNKS
-    order = sorted(range(2, workers), key=lambda o: (-bin(o // 2).count("1"), o // 2, o % 2)) + [1, 0]
+    starts = [rows * cut // CUTS[-1] for cut in CUTS]
+    chunks = [pl.ds(a, b - a) for a, b in zip(starts, starts[1:])]
+    bits = max(chips.bit_length() - 1, 0)
+
+    def far(o):
+        return bin(o // 2).count("1")
+
+    order = sorted(range(2, workers), key=lambda o: (far(o), o // 2, o % 2)) + [1, 0]
+    near = [o for o in range(1, workers) if far(o) < 2]
     peer = [flip(me, o, workers) for o in range(workers)]
 
     barrier = pltpu.get_barrier_semaphore()
-    for o in range(1, workers):
+    for o in near:
         pl.semaphore_signal(barrier, inc=1, device_id={"worker": peer[o]}, device_id_type=MESH)
-    for z in range(1, planes):
-        pl.semaphore_signal(
-            barrier, inc=1, device_id={"mp": (plane + z) % planes}, device_id_type=MESH
-        )
-
-    def load(o, c):
-        first = pl.multiple_of(peer[o] * rows + c * span, span)
-        return pltpu.make_async_copy(
-            g_ref.at[pl.ds(first, span), :],
-            stage.at[o, pl.ds(c * span, span), :],
-            load_sem.at[o, c],
-        )
-
-    for c in range(CHUNKS):
+    below, above = plane > 0, plane < planes - 1
+    for there, step in ((below, -1), (above, 1)):
+
+        @pl.when(there)
+        def _(step=step):
+            pl.semaphore_signal(
+                barrier, inc=1, device_id={"mp": plane + step}, device_id_type=MESH
+            )
+
+    entered = len(near) + below.astype(jnp.int32) + above.astype(jnp.int32)
+
+    def tell_chips(distance):
+        for b in range(bits - distance):
+            pl.semaphore_signal(
+                chip_hello.at[distance - 1],
+                inc=1,
+                device_id={"worker": peer[2 << b]},
+                device_id_type=MESH,
+            )
+
+    def hear_chips(distance):
+        if bits > distance:
+            pl.semaphore_wait(chip_hello.at[distance - 1], bits - distance)
+
+    def tell(distance):
+        if distance > planes - 2:
+            return
+        for n, step in ((0, -1), (1, 1)):
+            to, seen = plane + step, plane - step * distance
+
+            @pl.when((0 <= to) & (to < planes) & (0 <= seen) & (seen < planes))
+            def _(n=n, to=to):
+                pl.semaphore_signal(
+                    hello.at[n, distance - 1], inc=1, device_id={"mp": to}, device_id_type=MESH
+                )
+
+    def hear(distance):
+        for n, step in ((0, 1), (1, -1)):
+            seen = plane + step * (distance + 1)
+
+            @pl.when((0 <= seen) & (seen < planes))
+            def _(n=n):
+                pl.semaphore_wait(hello.at[n, distance - 1], 1)
+
+    for c, at in enumerate(chunks):
         for o in order:
-            load(o, c).start()
+            first = pl.multiple_of(peer[o] * rows, rows) + at.start
+            pltpu.make_async_copy(
+                g_ref.at[pl.ds(first, at.size), :], stage.at[o, at, :], load_sem.at[c]
+            ).start()
     lists = pltpu.make_async_copy(nb_hbm, nb_ref, small_sem)
     lists.start()
 
-    def gram_copy(o, c, slot):
-        at = pl.ds(c * span, span)
+    def to_peer(o, src, dst, send_sem, recv_sem):
         return pltpu.make_async_remote_copy(
-            src_ref=rounded.at[o, at, :],
-            dst_ref=recv.at[slot, at, :],
-            send_sem=gsend.at[o, c],
-            recv_sem=grecv.at[o, c],
+            src_ref=src,
+            dst_ref=dst,
+            send_sem=send_sem,
+            recv_sem=recv_sem,
             device_id={"worker": peer[o]},
             device_id_type=MESH,
         )
 
+    def gram_copy(o, c):
+        at = chunks[c]
+        return to_peer(o, rounded.at[o, at, :], recv.at[me, at, :], gsend, grecv.at[c])
+
+    def gram_chunk(c):
+        whole = recv.at[pl.ds(0, workers - 1), chunks[c], :]
+        return to_peer(1, whole, whole, gsend, grecv.at[c])
+
     keep = jnp.where(win_ref[0] == me, 1.0, 0.0).astype(jnp.float32)
 
-    def convert(o, c):
-        at = pl.ds(c * span, span)
+    def convert(o, at):
         x = stage[o, at, :]
         hi = x.astype(jnp.bfloat16)
         if o == 0:
@@ -114,71 +166,83 @@
 
     def swap(ox):
         there = flip(chip, ox, chips)
-        return pltpu.make_async_remote_copy(
-            src_ref=rest.at[1 - core, there],
-            dst_ref=rest_in.at[there],
-            send_sem=osend.at[ox],
-            recv_sem=orecv.at[ox],
-            device_id={"worker": peer[1]},
-            device_id_type=MESH,
-        )
+        return to_peer(1, rest.at[1 - core, there], rest_in.at[there], osend, orecv)
 
     def add_to_rest(there, at, other):
         rest_in[there, at, :] = rest_in[there, at, :] + other
 
     def combine(ox):
         there = flip(chip, ox, chips)
-        swap(ox).wait_recv()
-        for c in range(CHUNKS):
-            at = pl.ds(c * span, span)
+        for at in chunks:
             add_to_rest(there, at, rest[core, there, at, :])
 
     split = chips == 4
     half = rows // 2
-
-    def relay_copy(ox):
-        return pltpu.make_async_remote_copy(
-            src_ref=rest_in.at[flip(chip, 3, chips), pl.ds((ox - 1) * half, half), :],
-            dst_ref=relay.at[ox - 1],
-            send_sem=ysend.at[ox - 1],
-            recv_sem=yrecv.at[ox - 1],
-            device_id={"worker": peer[2 * ox]},
-            device_id_type=MESH,
+    piece = half // PIECES
+
+    def relay_copy(ox, p):
+        at = pl.ds(p * piece, piece)
+        return to_peer(
+            2 * ox,
+            rest_in.at[flip(chip, 3, chips), pl.ds((ox - 1) * half + p * piece, piece), :],
+            relay.at[ox - 1, at, :],
+            ysend,
+            yrecv.at[ox - 1, p],
         )
 
-    def rest_copy(ox, n):
-        at = pl.ds(n * half, half)
-        return pltpu.make_async_remote_copy(
-            src_ref=rest_in.at[flip(chip, ox, chips), at, :],
-            dst_ref=rest_recv.at[ox, at, :],
-            send_sem=rsend.at[ox, n],
-            recv_sem=rrecv.at[ox, n],
-            device_id={"worker": peer[2 * ox]},
-            device_id_type=MESH,
+    def rest_copy(ox, n, p):
+        at = pl.ds(n * half + p * piece, piece)
+        return to_peer(
+            2 * ox,
+            rest_in.at[flip(chip, ox, chips), at, :],
+            rest_recv.at[ox, at, :],
+            rsend,
+            rrecv,
         )
 
     rest_order = sorted(range(1, chips), key=lambda ox: bin(ox).count("1"))
     if split:
         rest_order = [1, 2]
 
-    first = True
-    for c in range(CHUNKS):
+    first, reach = True, 1
+    for c, at in enumerate(chunks):
+        pltpu.make_async_copy(stage.at[:, at, :], stage.at[:, at, :], load_sem.at[c]).wait()
         for o in order:
-            load(o, c).wait()
-            convert(o, c)
+            convert(o, at)
             if first:
-                pl.semaphore_wait(barrier, workers - 1 + planes - 1)
-                first = False
+              pl.semaphore_wait(barrier, entered)
+              tell_chips(1)
+              tell(1)
+              first = False
+            if c == 0 and far(o) > reach:
+                for distance in range(reach, far(o)):
+                  hear_chips(distance)
+                  tell_chips(distance + 1)
+                reach = far(o)
             if o:
-                gram_copy(o, c, me).start()
+                gram_copy(o, c).start()
     for ox in range(chips):
         swap(ox).start()
 
+    to_peer(1, rest_in, rest_in, osend, orecv).wait_recv()
+    for ox in reversed(range(chips)):
+        combine(ox)
+
+    def early(ox):
+        for p in range(PIECES):
+            relay_copy(ox, p).start()
+        for p in range(PIECES):
+            rest_copy(ox, ox - 1, p).start()
+
+    if split:
+        for n in EARLY[0]:
+            early(n)
+
     pairs = [(i, k) for i in range(workers) for k in range(i, workers)]
 
-    def gram(first, accs):
+    def gram(rows_at, accs):
         def one(step, accs):
-            at = pl.ds(pl.multiple_of(first + step * 16, 16), 16)
+            at = pl.ds(pl.multiple_of(rows_at.start + step * 16, 16), 16)
             xs = [recv[i, at, :].astype(jnp.float32) for i in range(workers)]
             lo = [x[:8] for x in xs]
             hi = [x[8:] for x in xs]
@@ -186,19 +250,23 @@
                 a + (lo[i] * lo[k] + hi[i] * hi[k]) for a, (i, k) in zip(accs, pairs)
             )
 
-        return lax.fori_loop(0, span // 16, one, accs)
+        return lax.fori_loop(0, rows_at.size // 16, one, accs)
 
     accs = tuple(jnp.zeros((8, LANES), jnp.float32) for _ in pairs)
-    for c in range(CHUNKS):
-        if c == CHUNKS - 1:
-            for ox in reversed(range(chips)):
-                combine(ox)
-            if split:
-                relay_copy(1).start()
-                relay_copy(2).start()
-        for o in order[:-1]:
-            gram_copy(o, c, peer[o]).wait_recv()
-        accs = gram(c * span, accs)
+    for c, at in enumerate(chunks):
+        if split and c == len(chunks) - 1:
+            for n in EARLY[1]:
+                early(n)
+        gram_chunk(c).wait_recv()
+        accs = gram(at, accs)
+        if c == 0:
+            for distance in range(1, planes - 1):
+                hear(distance)
+                tell(distance + 1)
+            for o in range(1, workers):
+                pl.semaphore_signal(
+                    lines, inc=1, device_id={"worker": peer[o]}, device_id_type=MESH
+                )
 
     value = dict(zip(pairs, accs))
     for i, k in pairs:
@@ -241,29 +309,32 @@
             device_id_type=MESH,
         )
 
+    pl.semaphore_wait(lines, workers - 1)
     for o in order:
         for z in range(planes):
             if o or z:
                 score_copy(o, z).start()
 
     if split:
-        for ox in rest_order:
-            rest_copy(ox, ox - 1).start()
-        for ox in rest_order:
-            relay_copy(ox).wait_recv()
-            add_to_rest(flip(chip, 3 - ox, chips), pl.ds((ox - 1) * half, half), relay[ox - 1])
-            rest_copy(3 - ox, ox - 1).start()
+        for n in EARLY[2]:
+            early(n)
+    if split:
+        for p in range(PIECES):
+            for ox in rest_order:
+                relay_copy(ox, p).wait_recv()
+                at = pl.ds((ox - 1) * half + p * piece, piece)
+                add_to_rest(flip(chip, 3 - ox, chips), at, relay[ox - 1, pl.ds(p * piece, piece), :])
+                rest_copy(3 - ox, ox - 1, p).start()
     else:
         for ox in rest_order:
             for n in range(2):
-                rest_copy(ox, n).start()
-
-    for n in range(2):
-        for ox in rest_order:
-            rest_copy(ox, n).wait_recv()
-
-    for c in range(CHUNKS):
-        at = pl.ds(c * span, span)
+                for p in range(PIECES):
+                    rest_copy(ox, n, p).start()
+
+    arrived = rest_recv.at[pl.ds(0, len(rest_order))]
+    to_peer(1, arrived, arrived, rsend, rrecv).wait_recv()
+
+    for at in chunks:
         low = rest_in[chip, at, :].astype(jnp.float32)
         for ox in rest_order:
             low = low + rest_recv[ox, at, :].astype(jnp.float32)
@@ -274,17 +345,12 @@
     scores_ref[...] = total[:, :workers]
 
     all_scores().wait_send()
-    for ox in range(chips):
-        swap(ox).wait_send()
+    to_peer(1, rest_in, rest_in, osend, orecv).wait_send()
     if split:
-        relay_copy(1).wait_send()
-        relay_copy(2).wait_send()
-    for o in order[:-1]:
-        for c in range(CHUNKS):
-            gram_copy(o, c, me).wait_send()
-    for ox in rest_order:
-        for n in range(2):
-            rest_copy(ox, n).wait_send()
+        to_peer(1, relay, relay, ysend, yrecv.at[0, 0]).wait_send()
+    sent = rounded.at[pl.ds(0, workers - 1)]
+    to_peer(1, sent, sent, gsend, grecv.at[0]).wait_send()
+    to_peer(1, arrived, arrived, rsend, rrecv).wait_send()
 
 
 def emit(scores_ref, block_ref, scores_out, block_out, sems):
@@ -337,17 +403,20 @@
                 pltpu.VMEM((workers, LANES), f32),
                 pltpu.VMEM((workers * planes, 1, LANES), f32),
                 dma,
-                dma((workers, CHUNKS)),
-                dma((workers, CHUNKS)),
-                dma((workers, CHUNKS)),
-                dma((chips,)),
-                dma((chips,)),
-                dma((2,)),
-                dma((2,)),
-                dma((chips, 2)),
-                dma((chips, 2)),
-                dma,
-                dma,
+                dma((len(CUTS) - 1,)),
+                dma,
+                dma((len(CUTS) - 1,)),
+                dma,
+                dma,
+                dma,
+                dma((2, PIECES)),
+                dma,
+                dma,
+                dma,
+                dma,
+                pltpu.SemaphoreType.REGULAR((2, max(planes - 2, 1))),
+                pltpu.SemaphoreType.REGULAR((max(chips.bit_length() - 2, 1),)),
+                pltpu.SemaphoreType.REGULAR,
             ],
             compiler_params=pltpu.CompilerParams(
                 collective_id=0, has_side_effects=True, vmem_limit_bytes=63_500_000

time: 27.5 us -> 25.4 us (0.924)
  Pallas kernels: 26 us -> 23.9 us
    pallas_call x1, Pallas kernels: 25.3 us -> 23.2 us  [body(): pl.pallas_call(functools.partial(kernel, workers, planes, entries), out_s...]
where the time goes in v2:
time: 25.4 us; the launch traced here: 25.2 us
  Pallas kernels  23.9 us (94%)
  between operations  1.28 us (5%)
    pallas_call x1, Pallas kernels, body(): pl.pallas_call(functools.partial(kernel, workers, planes, entries), out_s...  23.2 us
    pallas_call x1, Pallas kernels, body(): pl.pallas_call(emit, out_shape=(jax.ShapeDtypeStruct(scores.shape, f32),...  0.72 us

profile of v2, /device:TPU:0, one launch (start us, length us, event | category | flops | bytes accessed | tf_op | source)
XLA Modules:
  0.0 25.2 jit_solution(3535733420720807330)
XLA Ops:
  1.3 23.2 %shard_map.50 = (f32[1,8]{1,0:T(1,128)S(1)}, f32[512,128]{1,0:T(8,128)S(1)}) custom-call(s32[3,8]{1,0:T(4,128)} %bitcast.5, s32[1]{0:T(128)S(6)} %copy.5.win_ref, f32[4096,128]{1,0:T(8,128)} %bitcast.4), custom_call_target="tpu_custom_call" | custom-call | tf_op jit(solution)/shard_map/pallas_call | solution.py:378
  24.5 0.7 %shard_map.51 = (f32[1,8]{1,0:T(1,128)}, f32[512,128]{1,0:T(8,128)}) custom-call(f32[1,8]{1,0:T(1,128)S(1)} %get-tuple-element.6.scores_ref, f32[512,128]{1,0:T(8,128)S(1)} %get-tuple-element.7.block_ref), custom_call_target="tpu_custom_call" | custom-call | tf_op jit(solution)/shard_map/pallas_call | solution.py:425

commit v3 on v2

--- a/solution.py
+++ b/solution.py
@@ -9,9 +9,10 @@
 
 MESH = pl.DeviceIdType.MESH
 LANES = 128
-CUTS = (0, 2, 4, 6, 8)
+CHUNKS = 4
+SHIFT = 3 / 32
+TILE = 16
 PIECES = 2
-EARLY = ((), (1, 2), ())
 
 
 def flip(index, offset, size):
@@ -23,6 +24,12 @@
         result = result + digit * bit
         bit *= 2
     return result
+
+
+def cuts(rows, shift):
+    first = int(rows * SHIFT) // TILE * TILE if shift else 0
+    ends = [first + (rows - first) * n // CHUNKS // TILE * TILE for n in range(1, CHUNKS + 1)]
+    return ([0, first] if shift else [0]) + ends
 
 
 def kernel(
@@ -45,6 +52,8 @@
     dist,
     part,
     score_rows,
+    moved_in,
+    extra,
     small_sem,
     load_sem,
     gsend,
@@ -57,7 +66,11 @@
     rrecv,
     ssend,
     srecv,
-    hello,
+    zsend,
+    zrecv,
+    fsend,
+    frecv,
+    risen,
     chip_hello,
     lines,
 ):
@@ -67,8 +80,12 @@
     chip = me // 2
     chips = workers // 2
     rows = stage.shape[1]
-    starts = [rows * cut // CUTS[-1] for cut in CUTS]
+    split = chips == 4
+    shift = split and planes == 4
+    donor, helper, eager = planes - 1, planes - 3, 0
+    starts = cuts(rows, shift)
     chunks = [pl.ds(a, b - a) for a, b in zip(starts, starts[1:])]
+    moved = chunks[0]
     bits = max(chips.bit_length() - 1, 0)
 
     def far(o):
@@ -81,16 +98,13 @@
     barrier = pltpu.get_barrier_semaphore()
     for o in near:
         pl.semaphore_signal(barrier, inc=1, device_id={"worker": peer[o]}, device_id_type=MESH)
-    below, above = plane > 0, plane < planes - 1
-    for there, step in ((below, -1), (above, 1)):
-
-        @pl.when(there)
-        def _(step=step):
-            pl.semaphore_signal(
-                barrier, inc=1, device_id={"mp": plane + step}, device_id_type=MESH
-            )
-
-    entered = len(near) + below.astype(jnp.int32) + above.astype(jnp.int32)
+    for p in range(1, planes):
+
+        @pl.when(plane < p)
+        def _(p=p):
+            pl.semaphore_signal(barrier, inc=1, device_id={"mp": p}, device_id_type=MESH)
+
+    entered = len(near) + plane
 
     def tell_chips(distance):
         for b in range(bits - distance):
@@ -105,25 +119,12 @@
         if bits > distance:
             pl.semaphore_wait(chip_hello.at[distance - 1], bits - distance)
 
-    def tell(distance):
-        if distance > planes - 2:
-            return
-        for n, step in ((0, -1), (1, 1)):
-            to, seen = plane + step, plane - step * distance
-
-            @pl.when((0 <= to) & (to < planes) & (0 <= seen) & (seen < planes))
-            def _(n=n, to=to):
-                pl.semaphore_signal(
-                    hello.at[n, distance - 1], inc=1, device_id={"mp": to}, device_id_type=MESH
-                )
-
-    def hear(distance):
-        for n, step in ((0, 1), (1, -1)):
-            seen = plane + step * (distance + 1)
-
-            @pl.when((0 <= seen) & (seen < planes))
-            def _(n=n):
-                pl.semaphore_wait(hello.at[n, distance - 1], 1)
+    def tell_below():
+        for p in range(planes - 1):
+
+            @pl.when(p < plane)
+            def _(p=p):
+                pl.semaphore_signal(risen, inc=1, device_id={"mp": p}, device_id_type=MESH)
 
     for c, at in enumerate(chunks):
         for o in order:
@@ -159,7 +160,7 @@
         hi = x.astype(jnp.bfloat16)
         if o == 0:
             recv[me, at, :] = hi
-        else:
+        if o or (shift and at is moved):
             rounded[o, at, :] = hi
         low = ((x - hi.astype(jnp.float32)) * keep).astype(jnp.bfloat16)
         rest[peer[o] % 2, peer[o] // 2, at, :] = low
@@ -176,7 +177,6 @@
         for at in chunks:
             add_to_rest(there, at, rest[core, there, at, :])
 
-    split = chips == 4
     half = rows // 2
     piece = half // PIECES
 
@@ -204,23 +204,60 @@
     if split:
         rest_order = [1, 2]
 
-    first, reach = True, 1
+    def send(c, peers):
+        def start():
+            for o in peers:
+                gram_copy(o, c).start()
+
+        if shift and c == 0:
+            pl.when(plane != donor)(start)
+        elif shift and c == len(chunks) - 1:
+            pl.when(plane != eager)(start)
+        else:
+            start()
+
+    def to_helper():
+        return pltpu.make_async_remote_copy(
+            src_ref=rounded.at[:, moved, :],
+            dst_ref=moved_in,
+            send_sem=zsend,
+            recv_sem=zrecv,
+            device_id={"mp": helper},
+            device_id_type=MESH,
+        )
+
+    close = [o for o in order if o and far(o) < 2]
+    distant = [o for o in order if far(o) >= 2]
+    lead = 2 if shift else 1
     for c, at in enumerate(chunks):
         pltpu.make_async_copy(stage.at[:, at, :], stage.at[:, at, :], load_sem.at[c]).wait()
         for o in order:
             convert(o, at)
-            if first:
-              pl.semaphore_wait(barrier, entered)
-              tell_chips(1)
-              tell(1)
-              first = False
-            if c == 0 and far(o) > reach:
-                for distance in range(reach, far(o)):
-                  hear_chips(distance)
-                  tell_chips(distance + 1)
-                reach = far(o)
-            if o:
-                gram_copy(o, c).start()
+        if c == 0:
+          pl.semaphore_wait(barrier, entered)
+          tell_chips(1)
+          tell_below()
+        send(c, close)
+        if c == lead - 1:
+          for distance in range(1, bits):
+              hear_chips(distance)
+              tell_chips(distance + 1)
+          for late in range(lead):
+              send(late, distant)
+        elif c >= lead:
+            send(c, distant)
+        if shift and c == 0:
+
+            @pl.when(plane == donor)
+            def _():
+                to_helper().start()
+    if shift:
+
+        @pl.when(plane == donor)
+        def _():
+            for o in close + distant:
+                gram_copy(o, 0).start()
+
     for ox in range(chips):
         swap(ox).start()
 
@@ -228,45 +265,95 @@
     for ox in reversed(range(chips)):
         combine(ox)
 
-    def early(ox):
+    def relay_piece(p):
+        for ox in rest_order:
+            relay_copy(ox, p).start()
+
+    def own_halves():
         for p in range(PIECES):
-            relay_copy(ox, p).start()
-        for p in range(PIECES):
-            rest_copy(ox, ox - 1, p).start()
-
-    if split:
-        for n in EARLY[0]:
-            early(n)
+            for ox in rest_order:
+                rest_copy(ox, ox - 1, p).start()
+
+    def pass_on(p):
+        for ox in rest_order:
+            relay_copy(ox, p).wait_recv()
+            at = pl.ds(p * piece, piece)
+            there = flip(chip, 3 - ox, chips)
+            add_to_rest(there, pl.ds((ox - 1) * half + p * piece, piece), relay[ox - 1, at, :])
+            rest_copy(3 - ox, ox - 1, p).start()
+
+    if shift:
+
+        @pl.when(plane == eager)
+        def _():
+            relay_piece(0)
+            for o in close + distant:
+                gram_copy(o, len(chunks) - 1).start()
 
     pairs = [(i, k) for i in range(workers) for k in range(i, workers)]
 
-    def gram(rows_at, accs):
+    def gram(ref, at, accs, active=None):
         def one(step, accs):
-            at = pl.ds(pl.multiple_of(rows_at.start + step * 16, 16), 16)
-            xs = [recv[i, at, :].astype(jnp.float32) for i in range(workers)]
+            part_at = pl.ds(pl.multiple_of(at.start + step * TILE, TILE), TILE)
+            xs = [ref[i, part_at, :].astype(jnp.float32) for i in range(workers)]
             lo = [x[:8] for x in xs]
             hi = [x[8:] for x in xs]
             return tuple(
                 a + (lo[i] * lo[k] + hi[i] * hi[k]) for a, (i, k) in zip(accs, pairs)
             )
 
-        return lax.fori_loop(0, rows_at.size // 16, one, accs)
+        steps = at.size // TILE
+        if active is not None:
+            steps = steps * active.astype(jnp.int32)
+        return lax.fori_loop(0, steps, one, accs)
+
+    def forward(o):
+        return to_peer(o, moved_in.at[o], extra.at[me], fsend, frecv)
+
+    def forwarded():
+        whole = extra.at[pl.ds(0, workers - 1)]
+        return to_peer(1, whole, whole, fsend, frecv)
 
     accs = tuple(jnp.zeros((8, LANES), jnp.float32) for _ in pairs)
     for c, at in enumerate(chunks):
+        if shift and c == len(chunks) - 2:
+
+            @pl.when(plane == helper)
+            def _():
+              to_helper().wait_recv()
+              for o in close + distant:
+                  forward(o).start()
+              extra[me] = moved_in[0]
+
         if split and c == len(chunks) - 1:
-            for n in EARLY[1]:
-                early(n)
-        gram_chunk(c).wait_recv()
-        accs = gram(at, accs)
+            if shift:
+                pl.when(plane != eager)(lambda: relay_piece(0))
+            else:
+                relay_piece(0)
+            for p in range(1, PIECES):
+                relay_piece(p)
+            own_halves()
+            if shift:
+                pl.when(plane == eager)(lambda: pass_on(0))
+        if shift and c == 0:
+          pl.when(plane != donor)(gram_chunk(c).wait_recv)
+          accs = gram(recv, at, accs, plane != donor)
+        else:
+          gram_chunk(c).wait_recv()
+          accs = gram(recv, at, accs)
         if c == 0:
-            for distance in range(1, planes - 1):
-                hear(distance)
-                tell(distance + 1)
+
+            @pl.when(plane < planes - 1)
+            def _():
+                pl.semaphore_wait(risen, planes - 1 - plane)
+
             for o in range(1, workers):
                 pl.semaphore_signal(
                     lines, inc=1, device_id={"worker": peer[o]}, device_id_type=MESH
                 )
+    if shift:
+      pl.when(plane == helper)(forwarded().wait_recv)
+      accs = gram(extra, pl.ds(0, moved.size), accs, plane == helper)
 
     value = dict(zip(pairs, accs))
     for i, k in pairs:
@@ -288,13 +375,13 @@
     mine = plane * workers + me
     score_rows[mine] = jnp.sum(jnp.where(line == lane, column, 0.0), axis=0, keepdims=True)
 
-    def score_copy(o, z):
+    def score_copy(o, to):
         return pltpu.make_async_remote_copy(
             src_ref=score_rows.at[mine],
             dst_ref=score_rows.at[mine],
             send_sem=ssend,
             recv_sem=srecv,
-            device_id={"worker": peer[o], "mp": (plane + z) % planes},
+            device_id={"worker": peer[o], "mp": to},
             device_id_type=MESH,
         )
 
@@ -310,21 +397,21 @@
         )
 
     pl.semaphore_wait(lines, workers - 1)
-    for o in order:
-        for z in range(planes):
-            if o or z:
-                score_copy(o, z).start()
+    for to in range(planes):
+        for o in order[:-1]:
+            score_copy(o, to).start()
+
+        @pl.when(plane != to)
+        def _(to=to):
+            score_copy(0, to).start()
 
     if split:
-        for n in EARLY[2]:
-            early(n)
-    if split:
-        for p in range(PIECES):
-            for ox in rest_order:
-                relay_copy(ox, p).wait_recv()
-                at = pl.ds((ox - 1) * half + p * piece, piece)
-                add_to_rest(flip(chip, 3 - ox, chips), at, relay[ox - 1, pl.ds(p * piece, piece), :])
-                rest_copy(3 - ox, ox - 1, p).start()
+        if shift:
+            pl.when(plane != eager)(lambda: pass_on(0))
+        else:
+            pass_on(0)
+        for p in range(1, PIECES):
+            pass_on(p)
     else:
         for ox in rest_order:
             for n in range(2):
@@ -334,6 +421,8 @@
     arrived = rest_recv.at[pl.ds(0, len(rest_order))]
     to_peer(1, arrived, arrived, rsend, rrecv).wait_recv()
 
+    if shift:
+        pl.when(plane == donor)(gram_chunk(0).wait_recv)
     for at in chunks:
         low = rest_in[chip, at, :].astype(jnp.float32)
         for ox in rest_order:
@@ -350,6 +439,9 @@
         to_peer(1, relay, relay, ysend, yrecv.at[0, 0]).wait_send()
     sent = rounded.at[pl.ds(0, workers - 1)]
     to_peer(1, sent, sent, gsend, grecv.at[0]).wait_send()
+    if shift:
+        pl.when(plane == donor)(to_helper().wait_send)
+        pl.when(plane == helper)(forwarded().wait_send)
     to_peer(1, arrived, arrived, rsend, rrecv).wait_send()
 
 
@@ -372,6 +464,7 @@
     def body(gradients, neighbours, winner):
         length = gradients.shape[1]
         rows = length // (LANES * workers)
+        starts = cuts(rows, chips == 4 and planes == 4)
         entries = neighbours.shape[1] * length * planes
         bf16, f32 = jnp.bfloat16, jnp.float32
         dma = pltpu.SemaphoreType.DMA
@@ -402,10 +495,12 @@
                 pltpu.VMEM((workers * workers, 8, LANES), f32),
                 pltpu.VMEM((workers, LANES), f32),
                 pltpu.VMEM((workers * planes, 1, LANES), f32),
-                dma,
-                dma((len(CUTS) - 1,)),
-                dma,
-                dma((len(CUTS) - 1,)),
+                pltpu.VMEM((workers, starts[1], LANES), bf16),
+                pltpu.VMEM((workers, starts[1], LANES), bf16),
+                dma,
+                dma((len(starts) - 1,)),
+                dma,
+                dma((len(starts) - 1,)),
                 dma,
                 dma,
                 dma,
@@ -414,7 +509,11 @@
                 dma,
                 dma,
                 dma,
-                pltpu.SemaphoreType.REGULAR((2, max(planes - 2, 1))),
+                dma,
+                dma,
+                dma,
+                dma,
+                pltpu.SemaphoreType.REGULAR,
                 pltpu.SemaphoreType.REGULAR((max(chips.bit_length() - 2, 1),)),
                 pltpu.SemaphoreType.REGULAR,
             ],

time: 25.4 us -> 24.9 us (0.980)
  Pallas kernels: 23.9 us -> 23.4 us
    pallas_call x1, Pallas kernels: 23.2 us -> 22.7 us  [body(): pl.pallas_call(functools.partial(kernel, workers, planes, entries), out_s...]
where the time goes in v3:
time: 24.9 us; the launch traced here: 24.7 us
  Pallas kernels  23.4 us (94%)
  between operations  1.28 us (5%)
    pallas_call x1, Pallas kernels, body(): pl.pallas_call(functools.partial(kernel, workers, planes, entries), out_s...  22.7 us
    pallas_call x1, Pallas kernels, body(): pl.pallas_call(emit, out_shape=(jax.ShapeDtypeStruct(scores.shape, f32),...  0.72 us

profile of v3, /device:TPU:0, one launch (start us, length us, event | category | flops | bytes accessed | tf_op | source)
XLA Modules:
  0.0 24.7 jit_solution(10003537094398880136)
XLA Ops:
  1.3 22.7 %shard_map.50 = (f32[1,8]{1,0:T(1,128)S(1)}, f32[512,128]{1,0:T(8,128)S(1)}) custom-call(s32[3,8]{1,0:T(4,128)} %bitcast.5, s32[1]{0:T(128)S(6)} %copy.5.win_ref, f32[4096,128]{1,0:T(8,128)} %bitcast.4), custom_call_target="tpu_custom_call" | custom-call | tf_op jit(solution)/shard_map/pallas_call | solution.py:471
  24.0 0.7 %shard_map.51 = (f32[1,8]{1,0:T(1,128)}, f32[512,128]{1,0:T(8,128)}) custom-call(f32[1,8]{1,0:T(1,128)S(1)} %get-tuple-element.6.scores_ref, f32[512,128]{1,0:T(8,128)S(1)} %get-tuple-element.7.block_ref), custom_call_target="tpu_custom_call" | custom-call | tf_op jit(solution)/shard_map/pallas_call | solution.py:524

commit v4 on v3

--- a/solution.py
+++ b/solution.py
@@ -10,7 +10,8 @@
 MESH = pl.DeviceIdType.MESH
 LANES = 128
 CHUNKS = 4
-SHIFT = 3 / 32
+SHARES = (1, 2)
+PARTS = 32
 TILE = 16
 PIECES = 2
 
@@ -26,10 +27,15 @@
     return result
 
 
-def cuts(rows, shift):
-    first = int(rows * SHIFT) // TILE * TILE if shift else 0
+def shares(rows, chips, planes):
+    unit = rows // PARTS // TILE * TILE
+    return [unit * n for n in SHARES] if chips == planes == 4 and unit else []
+
+
+def cuts(rows, given):
+    first = sum(given)
     ends = [first + (rows - first) * n // CHUNKS // TILE * TILE for n in range(1, CHUNKS + 1)]
-    return ([0, first] if shift else [0]) + ends
+    return ([0, first] if first else [0]) + ends
 
 
 def kernel(
@@ -81,9 +87,10 @@
     chips = workers // 2
     rows = stage.shape[1]
     split = chips == 4
-    shift = split and planes == 4
-    donor, helper, eager = planes - 1, planes - 3, 0
-    starts = cuts(rows, shift)
+    given = shares(rows, chips, planes)
+    shift = bool(given)
+    donor, eager = planes - 1, 0
+    starts = cuts(rows, given)
     chunks = [pl.ds(a, b - a) for a, b in zip(starts, starts[1:])]
     moved = chunks[0]
     bits = max(chips.bit_length() - 1, 0)
@@ -126,7 +133,9 @@
             def _(p=p):
                 pl.semaphore_signal(risen, inc=1, device_id={"mp": p}, device_id_type=MESH)
 
-    for c, at in enumerate(chunks):
+    turns = [1, 0] + list(range(2, len(chunks))) if shift else list(range(len(chunks)))
+    for c in turns:
+        at = chunks[c]
         for o in order:
             first = pl.multiple_of(peer[o] * rows, rows) + at.start
             pltpu.make_async_copy(
@@ -216,41 +225,46 @@
         else:
             start()
 
-    def to_helper():
+    def to_helper(p):
         return pltpu.make_async_remote_copy(
-            src_ref=rounded.at[:, moved, :],
-            dst_ref=moved_in,
+            src_ref=rounded.at[:, pl.ds(sum(given[:p]), given[p]), :],
+            dst_ref=moved_in.at[:, pl.ds(0, given[p]), :],
             send_sem=zsend,
             recv_sem=zrecv,
-            device_id={"mp": helper},
+            device_id={"mp": p},
             device_id_type=MESH,
         )
 
     close = [o for o in order if o and far(o) < 2]
     distant = [o for o in order if far(o) >= 2]
     lead = 2 if shift else 1
-    for c, at in enumerate(chunks):
+    for turn, c in enumerate(turns):
+        at = chunks[c]
         pltpu.make_async_copy(stage.at[:, at, :], stage.at[:, at, :], load_sem.at[c]).wait()
         for o in order:
             convert(o, at)
-        if c == 0:
-          pl.semaphore_wait(barrier, entered)
-          tell_chips(1)
-          tell_below()
-        send(c, close)
-        if c == lead - 1:
-          for distance in range(1, bits):
-              hear_chips(distance)
-              tell_chips(distance + 1)
-          for late in range(lead):
-              send(late, distant)
-        elif c >= lead:
-            send(c, distant)
+            if turn == 0 and o == order[0]:
+                pl.semaphore_wait(barrier, entered)
+                tell_chips(1)
+                tell_below()
+            if turn == 0 and o in close:
+                gram_copy(o, c).start()
+        if turn and turn < lead:
+            send(c, close)
+        elif turn >= lead:
+            send(c, distant + close)
+        if turn == lead - 1:
+            for distance in range(1, bits):
+                hear_chips(distance)
+                tell_chips(distance + 1)
+            for late in turns[:lead]:
+                send(late, distant)
         if shift and c == 0:
 
             @pl.when(plane == donor)
             def _():
-                to_helper().start()
+                for p in range(len(given)):
+                    to_helper(p).start()
     if shift:
 
         @pl.when(plane == donor)
@@ -307,23 +321,27 @@
             steps = steps * active.astype(jnp.int32)
         return lax.fori_loop(0, steps, one, accs)
 
-    def forward(o):
-        return to_peer(o, moved_in.at[o], extra.at[me], fsend, frecv)
-
-    def forwarded():
-        whole = extra.at[pl.ds(0, workers - 1)]
+    def forward(o, p):
+        at = pl.ds(0, given[p])
+        return to_peer(o, moved_in.at[o, at, :], extra.at[me, at, :], fsend, frecv)
+
+    def forwarded(p):
+        whole = extra.at[pl.ds(0, workers - 1), pl.ds(0, given[p]), :]
         return to_peer(1, whole, whole, fsend, frecv)
 
     accs = tuple(jnp.zeros((8, LANES), jnp.float32) for _ in pairs)
     for c, at in enumerate(chunks):
         if shift and c == len(chunks) - 2:
 
-            @pl.when(plane == helper)
-            def _():
-              to_helper().wait_recv()
-              for o in close + distant:
-                  forward(o).start()
-              extra[me] = moved_in[0]
+            for p in range(len(given)):
+
+                @pl.when(plane == p)
+                def _(p=p):
+                    to_helper(p).wait_recv()
+                    for o in close + distant:
+                        forward(o, p).start()
+                    at = pl.ds(0, given[p])
+                    extra[me, at, :] = moved_in[0, at, :]
 
         if split and c == len(chunks) - 1:
             if shift:
@@ -352,8 +370,9 @@
                     lines, inc=1, device_id={"worker": peer[o]}, device_id_type=MESH
                 )
     if shift:
-      pl.when(plane == helper)(forwarded().wait_recv)
-      accs = gram(extra, pl.ds(0, moved.size), accs, plane == helper)
+      for p in range(len(given)):
+          pl.when(plane == p)(forwarded(p).wait_recv)
+          accs = gram(extra, pl.ds(0, given[p]), accs, plane == p)
 
     value = dict(zip(pairs, accs))
     for i, k in pairs:
@@ -440,8 +459,15 @@
     sent = rounded.at[pl.ds(0, workers - 1)]
     to_peer(1, sent, sent, gsend, grecv.at[0]).wait_send()
     if shift:
-        pl.when(plane == donor)(to_helper().wait_send)
-        pl.when(plane == helper)(forwarded().wait_send)
+
+        @pl.when(plane == donor)
+        def _():
+            whole = rounded.at[:, moved, :]
+            to_peer(1, whole, whole, zsend, zrecv).wait_send()
+
+        for p in range(len(given)):
+            pl.when(plane == p)(forwarded(p).wait_send)
+
     to_peer(1, arrived, arrived, rsend, rrecv).wait_send()
 
 
@@ -464,7 +490,8 @@
     def body(gradients, neighbours, winner):
         length = gradients.shape[1]
         rows = length // (LANES * workers)
-        starts = cuts(rows, chips == 4 and planes == 4)
+        given = shares(rows, chips, planes)
+        starts = cuts(rows, given)
         entries = neighbours.shape[1] * length * planes
         bf16, f32 = jnp.bfloat16, jnp.float32
         dma = pltpu.SemaphoreType.DMA
@@ -495,8 +522,8 @@
                 pltpu.VMEM((workers * workers, 8, LANES), f32),
                 pltpu.VMEM((workers, LANES), f32),
                 pltpu.VMEM((workers * planes, 1, LANES), f32),
-                pltpu.VMEM((workers, starts[1], LANES), bf16),
-                pltpu.VMEM((workers, starts[1], LANES), bf16),
+                pltpu.VMEM((workers, max(given + [TILE]), LANES), bf16),
+                pltpu.VMEM((workers, max(given + [TILE]), LANES), bf16),
                 dma,
                 dma((len(starts) - 1,)),
                 dma,

time: 24.9 us -> 24.8 us (level)
  no operation moved by 1% of the time
where the time goes in v4:
time: 24.8 us; the launch traced here: 24.6 us
  Pallas kernels  23.3 us (94%)
  between operations  1.28 us (5%)
    pallas_call x1, Pallas kernels, body(): pl.pallas_call(functools.partial(kernel, workers, planes, entries), out_s...  22.6 us
    pallas_call x1, Pallas kernels, body(): pl.pallas_call(emit, out_shape=(jax.ShapeDtypeStruct(scores.shape, f32),...  0.72 us

profile of v4, /device:TPU:0, one launch (start us, length us, event | category | flops | bytes accessed | tf_op | source)
XLA Modules:
  0.0 24.6 jit_solution(1618704295931833915)
XLA Ops:
  1.3 22.6 %shard_map.50 = (f32[1,8]{1,0:T(1,128)S(1)}, f32[512,128]{1,0:T(8,128)S(1)}) custom-call(s32[3,8]{1,0:T(4,128)} %bitcast.5, s32[1]{0:T(128)S(6)} %copy.5.win_ref, f32[4096,128]{1,0:T(8,128)} %bitcast.4), custom_call_target="tpu_custom_call" | custom-call | tf_op jit(solution)/shard_map/pallas_call | solution.py:498
  23.9 0.7 %shard_map.51 = (f32[1,8]{1,0:T(1,128)}, f32[512,128]{1,0:T(8,128)}) custom-call(f32[1,8]{1,0:T(1,128)S(1)} %get-tuple-element.6.scores_ref, f32[512,128]{1,0:T(8,128)S(1)} %get-tuple-element.7.block_ref), custom_call_target="tpu_custom_call" | custom-call | tf_op jit(solution)/shard_map/pallas_call | solution.py:551

commit v5 on v4

--- a/solution.py
+++ b/solution.py
@@ -62,19 +62,14 @@
     extra,
     small_sem,
     load_sem,
-    gsend,
+    sent_sem,
     grecv,
-    osend,
     orecv,
-    ysend,
     yrecv,
-    rsend,
     rrecv,
     ssend,
     srecv,
-    zsend,
     zrecv,
-    fsend,
     frecv,
     risen,
     chip_hello,
@@ -139,7 +134,7 @@
         for o in order:
             first = pl.multiple_of(peer[o] * rows, rows) + at.start
             pltpu.make_async_copy(
-                g_ref.at[pl.ds(first, at.size), :], stage.at[o, at, :], load_sem.at[c]
+                g_ref.at[pl.ds(first, at.size), :], stage.at[o, at, :], load_sem.at[min(c, len(chunks) - 2)]
             ).start()
     lists = pltpu.make_async_copy(nb_hbm, nb_ref, small_sem)
     lists.start()
@@ -156,11 +151,11 @@
 
     def gram_copy(o, c):
         at = chunks[c]
-        return to_peer(o, rounded.at[o, at, :], recv.at[me, at, :], gsend, grecv.at[c])
+        return to_peer(o, rounded.at[o, at, :], recv.at[me, at, :], sent_sem, grecv.at[c])
 
     def gram_chunk(c):
         whole = recv.at[pl.ds(0, workers - 1), chunks[c], :]
-        return to_peer(1, whole, whole, gsend, grecv.at[c])
+        return to_peer(1, whole, whole, sent_sem, grecv.at[c])
 
     keep = jnp.where(win_ref[0] == me, 1.0, 0.0).astype(jnp.float32)
 
@@ -176,7 +171,7 @@
 
     def swap(ox):
         there = flip(chip, ox, chips)
-        return to_peer(1, rest.at[1 - core, there], rest_in.at[there], osend, orecv)
+        return to_peer(1, rest.at[1 - core, there], rest_in.at[there], sent_sem, orecv)
 
     def add_to_rest(there, at, other):
         rest_in[there, at, :] = rest_in[there, at, :] + other
@@ -195,8 +190,8 @@
             2 * ox,
             rest_in.at[flip(chip, 3, chips), pl.ds((ox - 1) * half + p * piece, piece), :],
             relay.at[ox - 1, at, :],
-            ysend,
-            yrecv.at[ox - 1, p],
+            sent_sem,
+            yrecv.at[p],
         )
 
     def rest_copy(ox, n, p):
@@ -205,7 +200,7 @@
             2 * ox,
             rest_in.at[flip(chip, ox, chips), at, :],
             rest_recv.at[ox, at, :],
-            rsend,
+            sent_sem,
             rrecv,
         )
 
@@ -229,7 +224,7 @@
         return pltpu.make_async_remote_copy(
             src_ref=rounded.at[:, pl.ds(sum(given[:p]), given[p]), :],
             dst_ref=moved_in.at[:, pl.ds(0, given[p]), :],
-            send_sem=zsend,
+            send_sem=sent_sem,
             recv_sem=zrecv,
             device_id={"mp": p},
             device_id_type=MESH,
@@ -240,7 +235,10 @@
     lead = 2 if shift else 1
     for turn, c in enumerate(turns):
         at = chunks[c]
-        pltpu.make_async_copy(stage.at[:, at, :], stage.at[:, at, :], load_sem.at[c]).wait()
+        if c < len(chunks) - 1:
+            end = rows if c == len(chunks) - 2 else starts[c + 1]
+            loaded = stage.at[:, pl.ds(at.start, end - at.start), :]
+            pltpu.make_async_copy(loaded, loaded, load_sem.at[c]).wait()
         for o in order:
             convert(o, at)
             if turn == 0 and o == order[0]:
@@ -275,7 +273,7 @@
     for ox in range(chips):
         swap(ox).start()
 
-    to_peer(1, rest_in, rest_in, osend, orecv).wait_recv()
+    to_peer(1, rest_in, rest_in, sent_sem, orecv).wait_recv()
     for ox in reversed(range(chips)):
         combine(ox)
 
@@ -289,9 +287,9 @@
                 rest_copy(ox, ox - 1, p).start()
 
     def pass_on(p):
+        at = pl.ds(p * piece, piece)
+        to_peer(1, relay.at[:, at, :], relay.at[:, at, :], sent_sem, yrecv.at[p]).wait_recv()
         for ox in rest_order:
-            relay_copy(ox, p).wait_recv()
-            at = pl.ds(p * piece, piece)
             there = flip(chip, 3 - ox, chips)
             add_to_rest(there, pl.ds((ox - 1) * half + p * piece, piece), relay[ox - 1, at, :])
             rest_copy(3 - ox, ox - 1, p).start()
@@ -323,11 +321,11 @@
 
     def forward(o, p):
         at = pl.ds(0, given[p])
-        return to_peer(o, moved_in.at[o, at, :], extra.at[me, at, :], fsend, frecv)
+        return to_peer(o, moved_in.at[o, at, :], extra.at[me, at, :], sent_sem, frecv)
 
     def forwarded(p):
         whole = extra.at[pl.ds(0, workers - 1), pl.ds(0, given[p]), :]
-        return to_peer(1, whole, whole, fsend, frecv)
+        return to_peer(1, whole, whole, sent_sem, frecv)
 
     accs = tuple(jnp.zeros((8, LANES), jnp.float32) for _ in pairs)
     for c, at in enumerate(chunks):
@@ -438,7 +436,7 @@
                     rest_copy(ox, n, p).start()
 
     arrived = rest_recv.at[pl.ds(0, len(rest_order))]
-    to_peer(1, arrived, arrived, rsend, rrecv).wait_recv()
+    to_peer(1, arrived, arrived, sent_sem, rrecv).wait_recv()
 
     if shift:
         pl.when(plane == donor)(gram_chunk(0).wait_recv)
@@ -453,22 +451,22 @@
     scores_ref[...] = total[:, :workers]
 
     all_scores().wait_send()
-    to_peer(1, rest_in, rest_in, osend, orecv).wait_send()
+    to_peer(1, rest_in, rest_in, sent_sem, orecv).wait_send()
     if split:
-        to_peer(1, relay, relay, ysend, yrecv.at[0, 0]).wait_send()
+        to_peer(1, relay, relay, sent_sem, yrecv.at[0]).wait_send()
     sent = rounded.at[pl.ds(0, workers - 1)]
-    to_peer(1, sent, sent, gsend, grecv.at[0]).wait_send()
+    to_peer(1, sent, sent, sent_sem, grecv.at[0]).wait_send()
     if shift:
 
         @pl.when(plane == donor)
         def _():
             whole = rounded.at[:, moved, :]
-            to_peer(1, whole, whole, zsend, zrecv).wait_send()
+            to_peer(1, whole, whole, sent_sem, zrecv).wait_send()
 
         for p in range(len(given)):
             pl.when(plane == p)(forwarded(p).wait_send)
 
-    to_peer(1, arrived, arrived, rsend, rrecv).wait_send()
+    to_peer(1, arrived, arrived, sent_sem, rrecv).wait_send()
 
 
 def emit(scores_ref, block_ref, scores_out, block_out, sems):
@@ -525,16 +523,11 @@
                 pltpu.VMEM((workers, max(given + [TILE]), LANES), bf16),
                 pltpu.VMEM((workers, max(given + [TILE]), LANES), bf16),
                 dma,
+                dma((len(starts) - 2,)),
+                dma,
                 dma((len(starts) - 1,)),
                 dma,
-                dma((len(starts) - 1,)),
-                dma,
-                dma,
-                dma,
-                dma((2, PIECES)),
-                dma,
-                dma,
-                dma,
+                dma((PIECES,)),
                 dma,
                 dma,
                 dma,

time: 24.8 us -> 24.7 us (level)
  no operation moved by 1% of the time
where the time goes in v5:
time: 24.7 us; the launch traced here: 24.5 us
  Pallas kernels  23.2 us (94%)
  between operations  1.28 us (5%)
    pallas_call x1, Pallas kernels, body(): pl.pallas_call(functools.partial(kernel, workers, planes, entries), out_s...  22.5 us
    pallas_call x1, Pallas kernels, body(): pl.pallas_call(emit, out_shape=(jax.ShapeDtypeStruct(scores.shape, f32),...  0.72 us

profile of v5, /device:TPU:0, one launch (start us, length us, event | category | flops | bytes accessed | tf_op | source)
XLA Modules:
  0.0 24.5 jit_solution(6887186886803256421)
XLA Ops:
  1.3 22.5 %shard_map.50 = (f32[1,8]{1,0:T(1,128)S(1)}, f32[512,128]{1,0:T(8,128)S(1)}) custom-call(s32[3,8]{1,0:T(4,128)} %bitcast.5, s32[1]{0:T(128)S(6)} %copy.5.win_ref, f32[4096,128]{1,0:T(8,128)} %bitcast.4), custom_call_target="tpu_custom_call" | custom-call | tf_op jit(solution)/shard_map/pallas_call | solution.py:496
  23.8 0.7 %shard_map.51 = (f32[1,8]{1,0:T(1,128)}, f32[512,128]{1,0:T(8,128)}) custom-call(f32[1,8]{1,0:T(1,128)S(1)} %get-tuple-element.6.scores_ref, f32[512,128]{1,0:T(8,128)S(1)} %get-tuple-element.7.block_ref), custom_call_target="tpu_custom_call" | custom-call | tf_op jit(solution)/shard_map/pallas_call | solution.py:544

commit v6 on v5

--- a/solution.py
+++ b/solution.py
@@ -374,9 +374,7 @@
 
     value = dict(zip(pairs, accs))
     for i, k in pairs:
-        if i == k:
-            dist[i * workers + i] = jnp.zeros((8, LANES), jnp.float32)
-        else:
+        if i < k:
             d = value[i, i] + value[k, k] - 2.0 * value[i, k]
             dist[i * workers + k] = d
             dist[k * workers + i] = d
@@ -415,7 +413,7 @@
 
     pl.semaphore_wait(lines, workers - 1)
     for to in range(planes):
-        for o in order[:-1]:
+        for o in distant + close:
             score_copy(o, to).start()
 
         @pl.when(plane != to)

time: 24.7 us -> 24.7 us (level)
  no operation moved by 1% of the time
where the time goes in v6:
time: 24.7 us; the launch traced here: 24.5 us
  Pallas kernels  23.2 us (94%)
  between operations  1.28 us (5%)
    pallas_call x1, Pallas kernels, body(): pl.pallas_call(functools.partial(kernel, workers, planes, entries), out_s...  22.5 us
    pallas_call x1, Pallas kernels, body(): pl.pallas_call(emit, out_shape=(jax.ShapeDtypeStruct(scores.shape, f32),...  0.72 us

profile of v6, /device:TPU:0, one launch (start us, length us, event | category | flops | bytes accessed | tf_op | source)
XLA Modules:
  0.0 24.5 jit_solution(18043186893772009813)
XLA Ops:
  1.3 22.5 %shard_map.50 = (f32[1,8]{1,0:T(1,128)S(1)}, f32[512,128]{1,0:T(8,128)S(1)}) custom-call(s32[3,8]{1,0:T(4,128)} %bitcast.5, s32[1]{0:T(128)S(6)} %copy.5.win_ref, f32[4096,128]{1,0:T(8,128)} %bitcast.4), custom_call_target="tpu_custom_call" | custom-call | tf_op jit(solution)/shard_map/pallas_call | solution.py:494
  23.7 0.7 %shard_map.51 = (f32[1,8]{1,0:T(1,128)}, f32[512,128]{1,0:T(8,128)}) custom-call(f32[1,8]{1,0:T(1,128)S(1)} %get-tuple-element.6.scores_ref, f32[512,128]{1,0:T(8,128)S(1)} %get-tuple-element.7.block_ref), custom_call_target="tpu_custom_call" | custom-call | tf_op jit(solution)/shard_map/pallas_call | solution.py:542
